TPU v7x, 8 devices: a whole 2x2x1 slice. The times are simulated.
8 devices in a mesh: rep: 1 (over z), pp: 8 (over x, y, core).
Axes of the slice: x: 2, y: 2, z: 1, core: 2. Of those that a mesh axis runs over, the one named last changes fastest.
Arguments:
- x: bfloat16 [16, 512, 512], P('rep')
- dy: bfloat16 [16, 512, 512], P('rep')
- w_gate: bfloat16 [8, 512, 1280], P('pp')
- w_up: bfloat16 [8, 512, 1280], P('pp')
- w_down: bfloat16 [8, 1280, 512], P('pp')
Outputs:
- output 1: bfloat16 [8, 512, 1280], P(('rep', 'pp'))
- output 2: bfloat16 [8, 512, 1280], P(('rep', 'pp'))
- output 3: bfloat16 [8, 1280, 512], P(('rep', 'pp'))
All inputs are finite; a program needn't handle non-finite values.
Results may differ from a plain program's by a relative error of at most 0.0266.
Values are sent between devices in bfloat16 or wider.
A program may use at most 2 GiB of HBM per device.

v0:
```python
import jax
import jax.numpy as jnp
from jax import lax
from jax.sharding import PartitionSpec as P

NAMES = ("w_gate", "w_up", "w_down")


def matmul(a, w):
    return jnp.dot(a, w, preferred_element_type=jnp.float32).astype(jnp.bfloat16)


def normed(h):
    wide = h.astype(jnp.float32)
    scale = lax.rsqrt(jnp.mean(wide**2, -1, keepdims=True) + 1e-6)
    return (wide * scale).astype(jnp.bfloat16)


def layer(h, w):
    a = normed(h)
    gate = jnp.dot(a, w["w_gate"], preferred_element_type=jnp.float32)
    up = jnp.dot(a, w["w_up"], preferred_element_type=jnp.float32)
    return h + matmul((jax.nn.silu(gate) * up).astype(jnp.bfloat16), w["w_down"])


def stage(weights, h):
    for number in range(weights["w_gate"].shape[0]):
        h = layer(h, {name: w[number] for name, w in weights.items()})
    return h


def solution(mesh):
    stages = mesh.shape["pp"]
    onward = [(i, i + 1) for i in range(stages - 1)]
    back_again = [(i + 1, i) for i in range(stages - 1)]

    def step(x, dy, *arrays):
        weights = dict(zip(NAMES, arrays, strict=True))
        micro, me = x.shape[0], lax.axis_index("pp")
        kept, came = jnp.zeros_like(x), jnp.zeros_like(x[0])
        for t in range(micro + stages - 1):
            number = jnp.clip(t - me, 0, micro - 1)
            at_work = (t >= me) & (t - me < micro)
            h = jnp.where(me == 0, x[min(t, micro - 1)], came)
            was = lax.dynamic_index_in_dim(kept, number, 0, keepdims=False)
            kept = lax.dynamic_update_index_in_dim(kept, jnp.where(at_work, h, was), number, 0)
            came = lax.ppermute(stage(weights, h), "pp", onward)
        total = {name: jnp.zeros(w.shape, jnp.float32) for name, w in weights.items()}
        came, behind = jnp.zeros_like(x[0]), stages - 1 - me
        for t in range(micro + stages - 1):
            number = jnp.clip(t - behind, 0, micro - 1)
            at_work = (t >= behind) & (t - behind < micro)
            by_y = jnp.where(behind == 0, dy[min(t, micro - 1)], came)
            _, back = jax.vjp(stage, weights, lax.dynamic_index_in_dim(kept, number, 0, keepdims=False))
            by_w, by_h = back(by_y)
            total = {name: total[name] + jnp.where(at_work, by_w[name].astype(jnp.float32), 0.0) for name in NAMES}
            came = lax.ppermute(by_h, "pp", back_again)
        return tuple(total[name].astype(jnp.bfloat16) for name in NAMES)

    return jax.shard_map(
        step,
        mesh=mesh,
        in_specs=(P("rep", None, None),) * 2 + (P("pp", None, None),) * 3,
        out_specs=(P(("rep", "pp"), None, None),) * 3,
        check_vma=False,
    )
```

profile of v0, /device:TPU:5, one launch (start us, length us, event | category | flops | bytes accessed | tf_op | source)
XLA Modules:
  0.0 1077.0 jit_solution(9822147989501524373)
XLA Ops:
  14.1 6.1 collective-permute-done
  34.1 6.1 collective-permute-done.1
  48.8 5.3 collective-permute-start.2
  54.1 6.1 collective-permute-done.2
  69.9 5.3 collective-permute-start.3
  75.2 6.1 collective-permute-done.3
  90.9 5.5 collective-permute-start.4
  96.4 5.9 collective-permute-done.4
  117.3 6.1 collective-permute-done.5
  133.0 5.3 collective-permute-start.6
  138.3 6.1 collective-permute-done.6
  154.1 5.3 collective-permute-start.7
  159.4 6.1 collective-permute-done.7
  180.5 6.1 collective-permute-done.8
  196.2 5.5 collective-permute-start.9
  201.8 5.8 collective-permute-done.9
  217.1 5.4 collective-permute-start.10
  259.0 5.4 collective-permute-start.12
  280.0 5.8 collective-permute-start.13
  321.9 5.4 collective-permute-start.15
  342.8 5.4 collective-permute-start.16
  363.8 5.6 collective-permute-start.17
  384.8 5.4 collective-permute-start.18
  405.7 5.4 collective-permute-start.19
  426.7 5.4 collective-permute-start.20
  447.6 5.6 collective-permute-start.21
  485.6 7.9 collective-permute-done.22
  534.6 6.8 collective-permute-done.24
  561.2 6.7 collective-permute-done.25
  587.7 6.8 collective-permute-done.26
  614.5 6.5 collective-permute-done.27
  640.6 6.9 collective-permute-done.28
  667.2 6.8 collective-permute-done.29
  693.8 6.7 collective-permute-done.30
  720.4 6.5 collective-permute-done.31
  746.6 6.8 collective-permute-done.32
  773.1 6.8 collective-permute-done.33
  799.7 6.7 collective-permute-done.34
  826.4 6.5 collective-permute-done.35
  852.6 6.8 collective-permute-done.36
  879.1 6.8 collective-permute-done.37
  905.7 6.7 collective-permute-done.38
  932.4 6.5 collective-permute-done.39
  958.6 6.8 collective-permute-done.40
  985.2 6.8 collective-permute-done.41
  1011.7 6.7 collective-permute-done.42
  1038.3 6.6 collective-permute-done.43
  1059.7 16.8 %fusion.229 = bf16[1,1280,512]{2,1,0:T(8,128)(2,1)} fusion(f32[1280,512]{1,0:T(8,128)} %fusion.206, f32[1280,512]{1,0:T(8,128)} %fusion.204, f32[1280,512]{1,0:T(8,128)} %fusion.202, f32[1280,512]{1,0:T(8,128)} %fusion.200, f32[1280,512]{1,0:T(8,128)} %fusion.198, f32[1280,512]{1,0:T(8,128)} %fusion.196, f32[1280,512]{1,0:T(8,128)} %fusion.194, ...), kind=kOutput, calls=%fused_computation.412 | convolution fusion | flops 692060160 | bytes 64749568 | tf_op jit(solution)/shard_map/transpose(jvp())/dot_general | solution.py:10
  (558 shorter events, 766.8 us)
Async XLA Ops:
  10.4 9.7 collective-permute-start
  28.8 11.4 %collective-permute-start.1 = (bf16[512,512]{1,0:T(8,128)(2,1)}, bf16[512,512]{1,0:T(8,128)(2,1)S(1)}, u32[]{:S(2)}, u32[]{:S(2)}) collective-permute-start(bf16[512,512]{1,0:T(8,128)(2,1)} %fusion.1032), channel_id=1, source_target_pairs={{0,1},{1,2},{2,3},{3,4},{4,5},{5,6},{6,7}} | collective-permute-start | bytes 1572872 | tf_op jit(solution)/shard_map/ppermute | solution.py:47
  48.8 11.4 %collective-permute-start.2 = (bf16[512,512]{1,0:T(8,128)(2,1)}, bf16[512,512]{1,0:T(8,128)(2,1)S(1)}, u32[]{:S(2)}, u32[]{:S(2)}) collective-permute-start(bf16[512,512]{1,0:T(8,128)(2,1)} %fusion.1029), channel_id=1, source_target_pairs={{0,1},{1,2},{2,3},{3,4},{4,5},{5,6},{6,7}} | collective-permute-start | bytes 1572872 | tf_op jit(solution)/shard_map/ppermute | solution.py:47
  69.9 11.4 %collective-permute-start.3 = (bf16[512,512]{1,0:T(8,128)(2,1)}, bf16[512,512]{1,0:T(8,128)(2,1)S(1)}, u32[]{:S(2)}, u32[]{:S(2)}) collective-permute-start(bf16[512,512]{1,0:T(8,128)(2,1)} %fusion.1026), channel_id=1, source_target_pairs={{0,1},{1,2},{2,3},{3,4},{4,5},{5,6},{6,7}} | collective-permute-start | bytes 1572872 | tf_op jit(solution)/shard_map/ppermute | solution.py:47
  90.9 11.4 %collective-permute-start.4 = (bf16[512,512]{1,0:T(8,128)(2,1)}, bf16[512,512]{1,0:T(8,128)(2,1)S(1)}, u32[]{:S(2)}, u32[]{:S(2)}) collective-permute-start(bf16[512,512]{1,0:T(8,128)(2,1)} %fusion.1023), channel_id=1, source_target_pairs={{0,1},{1,2},{2,3},{3,4},{4,5},{5,6},{6,7}} | collective-permute-start | bytes 1572872 | tf_op jit(solution)/shard_map/ppermute | solution.py:47
  112.0 11.4 %collective-permute-start.5 = (bf16[512,512]{1,0:T(8,128)(2,1)}, bf16[512,512]{1,0:T(8,128)(2,1)S(1)}, u32[]{:S(2)}, u32[]{:S(2)}) collective-permute-start(bf16[512,512]{1,0:T(8,128)(2,1)} %fusion.1020), channel_id=1, source_target_pairs={{0,1},{1,2},{2,3},{3,4},{4,5},{5,6},{6,7}} | collective-permute-start | bytes 1572872 | tf_op jit(solution)/shard_map/ppermute | solution.py:47
  133.0 11.4 %collective-permute-start.6 = (bf16[512,512]{1,0:T(8,128)(2,1)}, bf16[512,512]{1,0:T(8,128)(2,1)S(1)}, u32[]{:S(2)}, u32[]{:S(2)}) collective-permute-start(bf16[512,512]{1,0:T(8,128)(2,1)} %fusion.1017), channel_id=1, source_target_pairs={{0,1},{1,2},{2,3},{3,4},{4,5},{5,6},{6,7}} | collective-permute-start | bytes 1572872 | tf_op jit(solution)/shard_map/ppermute | solution.py:47
  154.1 11.4 %collective-permute-start.7 = (bf16[512,512]{1,0:T(8,128)(2,1)}, bf16[512,512]{1,0:T(8,128)(2,1)S(1)}, u32[]{:S(2)}, u32[]{:S(2)}) collective-permute-start(bf16[512,512]{1,0:T(8,128)(2,1)} %fusion.1014), channel_id=1, source_target_pairs={{0,1},{1,2},{2,3},{3,4},{4,5},{5,6},{6,7}} | collective-permute-start | bytes 1572872 | tf_op jit(solution)/shard_map/ppermute | solution.py:47
  175.2 11.4 %collective-permute-start.8 = (bf16[512,512]{1,0:T(8,128)(2,1)}, bf16[512,512]{1,0:T(8,128)(2,1)S(1)}, u32[]{:S(2)}, u32[]{:S(2)}) collective-permute-start(bf16[512,512]{1,0:T(8,128)(2,1)} %fusion.1011), channel_id=1, source_target_pairs={{0,1},{1,2},{2,3},{3,4},{4,5},{5,6},{6,7}} | collective-permute-start | bytes 1572872 | tf_op jit(solution)/shard_map/ppermute | solution.py:47
  196.2 11.4 %collective-permute-start.9 = (bf16[512,512]{1,0:T(8,128)(2,1)}, bf16[512,512]{1,0:T(8,128)(2,1)}, u32[]{:S(2)}, u32[]{:S(2)}) collective-permute-start(bf16[512,512]{1,0:T(8,128)(2,1)} %fusion.1008), channel_id=1, source_target_pairs={{0,1},{1,2},{2,3},{3,4},{4,5},{5,6},{6,7}} | collective-permute-start | bytes 1572872 | tf_op jit(solution)/shard_map/ppermute | solution.py:47
  217.1 11.4 %copy-start.51 = (bf16[1,1280,512]{2,1,0:T(8,128)(2,1)S(1)}, bf16[1,1280,512]{2,1,0:T(8,128)(2,1)}, u32[]{:S(2)}) copy-start(bf16[1,1280,512]{2,1,0:T(8,128)(2,1)} %param.9) | copy-start | bytes 3932164
  217.1 14.4 %collective-permute-start.10 = (bf16[512,512]{1,0:T(8,128)(2,1)}, bf16[512,512]{1,0:T(8,128)(2,1)S(1)}, u32[]{:S(2)}, u32[]{:S(2)}) collective-permute-start(bf16[512,512]{1,0:T(8,128)(2,1)} %fusion.1005), channel_id=1, source_target_pairs={{0,1},{1,2},{2,3},{3,4},{4,5},{5,6},{6,7}} | collective-permute-start | bytes 1572872 | tf_op jit(solution)/shard_map/ppermute | solution.py:47
  241.0 8.5 collective-permute-start.11
  259.0 11.5 %collective-permute-start.12 = (bf16[512,512]{1,0:T(8,128)(2,1)}, bf16[512,512]{1,0:T(8,128)(2,1)S(1)}, u32[]{:S(2)}, u32[]{:S(2)}) collective-permute-start(bf16[512,512]{1,0:T(8,128)(2,1)} %fusion.999), channel_id=1, source_target_pairs={{0,1},{1,2},{2,3},{3,4},{4,5},{5,6},{6,7}} | collective-permute-start | bytes 1572872 | tf_op jit(solution)/shard_map/ppermute | solution.py:47
  280.0 11.8 %collective-permute-start.13 = (bf16[512,512]{1,0:T(8,128)(2,1)}, bf16[512,512]{1,0:T(8,128)(2,1)S(1)}, u32[]{:S(2)}, u32[]{:S(2)}) collective-permute-start(bf16[512,512]{1,0:T(8,128)(2,1)} %fusion.996), channel_id=1, source_target_pairs={{0,1},{1,2},{2,3},{3,4},{4,5},{5,6},{6,7}} | collective-permute-start | bytes 1572872 | tf_op jit(solution)/shard_map/ppermute | solution.py:47
  301.2 11.3 %collective-permute-start.14 = (bf16[512,512]{1,0:T(8,128)(2,1)}, bf16[512,512]{1,0:T(8,128)(2,1)S(1)}, u32[]{:S(2)}, u32[]{:S(2)}) collective-permute-start(bf16[512,512]{1,0:T(8,128)(2,1)} %fusion.993), channel_id=1, source_target_pairs={{0,1},{1,2},{2,3},{3,4},{4,5},{5,6},{6,7}} | collective-permute-start | bytes 1572872 | tf_op jit(solution)/shard_map/ppermute | solution.py:47
  321.9 11.5 %collective-permute-start.15 = (bf16[512,512]{1,0:T(8,128)(2,1)}, bf16[512,512]{1,0:T(8,128)(2,1)S(1)}, u32[]{:S(2)}, u32[]{:S(2)}) collective-permute-start(bf16[512,512]{1,0:T(8,128)(2,1)} %fusion.990), channel_id=1, source_target_pairs={{0,1},{1,2},{2,3},{3,4},{4,5},{5,6},{6,7}} | collective-permute-start | bytes 1572872 | tf_op jit(solution)/shard_map/ppermute | solution.py:47
  342.8 11.5 %collective-permute-start.16 = (bf16[512,512]{1,0:T(8,128)(2,1)}, bf16[512,512]{1,0:T(8,128)(2,1)S(1)}, u32[]{:S(2)}, u32[]{:S(2)}) collective-permute-start(bf16[512,512]{1,0:T(8,128)(2,1)} %fusion.987), channel_id=1, source_target_pairs={{0,1},{1,2},{2,3},{3,4},{4,5},{5,6},{6,7}} | collective-permute-start | bytes 1572872 | tf_op jit(solution)/shard_map/ppermute | solution.py:47
  363.8 11.5 %collective-permute-start.17 = (bf16[512,512]{1,0:T(8,128)(2,1)}, bf16[512,512]{1,0:T(8,128)(2,1)S(1)}, u32[]{:S(2)}, u32[]{:S(2)}) collective-permute-start(bf16[512,512]{1,0:T(8,128)(2,1)} %fusion.984), channel_id=1, source_target_pairs={{0,1},{1,2},{2,3},{3,4},{4,5},{5,6},{6,7}} | collective-permute-start | bytes 1572872 | tf_op jit(solution)/shard_map/ppermute | solution.py:47
  384.8 11.5 %collective-permute-start.18 = (bf16[512,512]{1,0:T(8,128)(2,1)}, bf16[512,512]{1,0:T(8,128)(2,1)S(1)}, u32[]{:S(2)}, u32[]{:S(2)}) collective-permute-start(bf16[512,512]{1,0:T(8,128)(2,1)} %fusion.981), channel_id=1, source_target_pairs={{0,1},{1,2},{2,3},{3,4},{4,5},{5,6},{6,7}} | collective-permute-start | bytes 1572872 | tf_op jit(solution)/shard_map/ppermute | solution.py:47
  405.7 11.5 %collective-permute-start.19 = (bf16[512,512]{1,0:T(8,128)(2,1)}, bf16[512,512]{1,0:T(8,128)(2,1)S(1)}, u32[]{:S(2)}, u32[]{:S(2)}) collective-permute-start(bf16[512,512]{1,0:T(8,128)(2,1)} %fusion.978), channel_id=1, source_target_pairs={{0,1},{1,2},{2,3},{3,4},{4,5},{5,6},{6,7}} | collective-permute-start | bytes 1572872 | tf_op jit(solution)/shard_map/ppermute | solution.py:47
  426.7 11.5 %collective-permute-start.20 = (bf16[512,512]{1,0:T(8,128)(2,1)}, bf16[512,512]{1,0:T(8,128)(2,1)S(1)}, u32[]{:S(2)}, u32[]{:S(2)}) collective-permute-start(bf16[512,512]{1,0:T(8,128)(2,1)} %fusion.975), channel_id=1, source_target_pairs={{0,1},{1,2},{2,3},{3,4},{4,5},{5,6},{6,7}} | collective-permute-start | bytes 1572872 | tf_op jit(solution)/shard_map/ppermute | solution.py:47
  447.6 11.5 %collective-permute-start.21 = (bf16[512,512]{1,0:T(8,128)(2,1)}, bf16[512,512]{1,0:T(8,128)(2,1)S(1)}, u32[]{:S(2)}, u32[]{:S(2)}) collective-permute-start(bf16[512,512]{1,0:T(8,128)(2,1)} %fusion.972), channel_id=1, source_target_pairs={{0,1},{1,2},{2,3},{3,4},{4,5},{5,6},{6,7}} | collective-permute-start | bytes 1572872 | tf_op jit(solution)/shard_map/ppermute | solution.py:47
  477.1 31.6 %copy-start.2 = (f32[512,1280]{1,0:T(8,128)}, f32[512,1280]{1,0:T(8,128)S(1)}, u32[]{:S(2)}) copy-start(f32[512,1280]{1,0:T(8,128)S(1)} %fusion.657) | copy-start | bytes 7864324
  479.4 26.5 %copy-start.4 = (f32[512,1280]{1,0:T(8,128)}, f32[512,1280]{1,0:T(8,128)S(1)}, u32[]{:S(2)}) copy-start(f32[512,1280]{1,0:T(8,128)S(1)} %fusion.546) | copy-start | bytes 7864324
  481.2 12.4 %copy-start.52 = (bf16[1,1280,512]{2,1,0:T(8,128)(2,1)S(1)}, bf16[1,1280,512]{2,1,0:T(8,128)(2,1)}, u32[]{:S(2)}) copy-start(bf16[1,1280,512]{2,1,0:T(8,128)(2,1)} %param.9) | copy-start | bytes 3932164
  481.2 12.3 %collective-permute-start.22 = (bf16[512,512]{1,0:T(8,128)(2,1)S(1)}, bf16[512,512]{1,0:T(8,128)(2,1)S(1)}, u32[]{:S(2)}, u32[]{:S(2)}) collective-permute-start(bf16[512,512]{1,0:T(8,128)(2,1)S(1)} %fusion.1304), channel_id=1, source_target_pairs={{1,0},{2,1},{3,2},{4,3},{5,4},{6,5},{7,6}} | collective-permute-start | bytes 1572872 | tf_op jit(solution)/shard_map/ppermute | solution.py:57
  503.5 11.4 %collective-permute-start.23 = (bf16[512,512]{1,0:T(8,128)(2,1)S(1)}, bf16[512,512]{1,0:T(8,128)(2,1)S(1)}, u32[]{:S(2)}, u32[]{:S(2)}) collective-permute-start(bf16[512,512]{1,0:T(8,128)(2,1)S(1)} %fusion.1303), channel_id=1, source_target_pairs={{1,0},{2,1},{3,2},{4,3},{5,4},{6,5},{7,6}} | collective-permute-start | bytes 1572872 | tf_op jit(solution)/shard_map/ppermute | solution.py:57
  530.1 11.4 %collective-permute-start.24 = (bf16[512,512]{1,0:T(8,128)(2,1)S(1)}, bf16[512,512]{1,0:T(8,128)(2,1)S(1)}, u32[]{:S(2)}, u32[]{:S(2)}) collective-permute-start(bf16[512,512]{1,0:T(8,128)(2,1)S(1)} %fusion.1302), channel_id=1, source_target_pairs={{1,0},{2,1},{3,2},{4,3},{5,4},{6,5},{7,6}} | collective-permute-start | bytes 1572872 | tf_op jit(solution)/shard_map/ppermute | solution.py:57
  556.6 11.4 %collective-permute-start.25 = (bf16[512,512]{1,0:T(8,128)(2,1)S(1)}, bf16[512,512]{1,0:T(8,128)(2,1)S(1)}, u32[]{:S(2)}, u32[]{:S(2)}) collective-permute-start(bf16[512,512]{1,0:T(8,128)(2,1)S(1)} %fusion.1301), channel_id=1, source_target_pairs={{1,0},{2,1},{3,2},{4,3},{5,4},{6,5},{7,6}} | collective-permute-start | bytes 1572872 | tf_op jit(solution)/shard_map/ppermute | solution.py:57
  583.0 11.4 %collective-permute-start.26 = (bf16[512,512]{1,0:T(8,128)(2,1)S(1)}, bf16[512,512]{1,0:T(8,128)(2,1)S(1)}, u32[]{:S(2)}, u32[]{:S(2)}) collective-permute-start(bf16[512,512]{1,0:T(8,128)(2,1)S(1)} %fusion.1300), channel_id=1, source_target_pairs={{1,0},{2,1},{3,2},{4,3},{5,4},{6,5},{7,6}} | collective-permute-start | bytes 1572872 | tf_op jit(solution)/shard_map/ppermute | solution.py:57
  609.5 11.4 %collective-permute-start.27 = (bf16[512,512]{1,0:T(8,128)(2,1)S(1)}, bf16[512,512]{1,0:T(8,128)(2,1)S(1)}, u32[]{:S(2)}, u32[]{:S(2)}) collective-permute-start(bf16[512,512]{1,0:T(8,128)(2,1)S(1)} %fusion.1299), channel_id=1, source_target_pairs={{1,0},{2,1},{3,2},{4,3},{5,4},{6,5},{7,6}} | collective-permute-start | bytes 1572872 | tf_op jit(solution)/shard_map/ppermute | solution.py:57
  636.0 11.4 %collective-permute-start.28 = (bf16[512,512]{1,0:T(8,128)(2,1)S(1)}, bf16[512,512]{1,0:T(8,128)(2,1)S(1)}, u32[]{:S(2)}, u32[]{:S(2)}) collective-permute-start(bf16[512,512]{1,0:T(8,128)(2,1)S(1)} %fusion.1298), channel_id=1, source_target_pairs={{1,0},{2,1},{3,2},{4,3},{5,4},{6,5},{7,6}} | collective-permute-start | bytes 1572872 | tf_op jit(solution)/shard_map/ppermute | solution.py:57
  662.5 11.4 %collective-permute-start.29 = (bf16[512,512]{1,0:T(8,128)(2,1)S(1)}, bf16[512,512]{1,0:T(8,128)(2,1)S(1)}, u32[]{:S(2)}, u32[]{:S(2)}) collective-permute-start(bf16[512,512]{1,0:T(8,128)(2,1)S(1)} %fusion.1297), channel_id=1, source_target_pairs={{1,0},{2,1},{3,2},{4,3},{5,4},{6,5},{7,6}} | collective-permute-start | bytes 1572872 | tf_op jit(solution)/shard_map/ppermute | solution.py:57
  689.0 11.4 %collective-permute-start.30 = (bf16[512,512]{1,0:T(8,128)(2,1)S(1)}, bf16[512,512]{1,0:T(8,128)(2,1)S(1)}, u32[]{:S(2)}, u32[]{:S(2)}) collective-permute-start(bf16[512,512]{1,0:T(8,128)(2,1)S(1)} %fusion.1296), channel_id=1, source_target_pairs={{1,0},{2,1},{3,2},{4,3},{5,4},{6,5},{7,6}} | collective-permute-start | bytes 1572872 | tf_op jit(solution)/shard_map/ppermute | solution.py:57
  715.5 11.4 %collective-permute-start.31 = (bf16[512,512]{1,0:T(8,128)(2,1)S(1)}, bf16[512,512]{1,0:T(8,128)(2,1)S(1)}, u32[]{:S(2)}, u32[]{:S(2)}) collective-permute-start(bf16[512,512]{1,0:T(8,128)(2,1)S(1)} %fusion.1295), channel_id=1, source_target_pairs={{1,0},{2,1},{3,2},{4,3},{5,4},{6,5},{7,6}} | collective-permute-start | bytes 1572872 | tf_op jit(solution)/shard_map/ppermute | solution.py:57
  742.0 11.4 %collective-permute-start.32 = (bf16[512,512]{1,0:T(8,128)(2,1)S(1)}, bf16[512,512]{1,0:T(8,128)(2,1)S(1)}, u32[]{:S(2)}, u32[]{:S(2)}) collective-permute-start(bf16[512,512]{1,0:T(8,128)(2,1)S(1)} %fusion.1294), channel_id=1, source_target_pairs={{1,0},{2,1},{3,2},{4,3},{5,4},{6,5},{7,6}} | collective-permute-start | bytes 1572872 | tf_op jit(solution)/shard_map/ppermute | solution.py:57
  768.5 11.4 %collective-permute-start.33 = (bf16[512,512]{1,0:T(8,128)(2,1)S(1)}, bf16[512,512]{1,0:T(8,128)(2,1)S(1)}, u32[]{:S(2)}, u32[]{:S(2)}) collective-permute-start(bf16[512,512]{1,0:T(8,128)(2,1)S(1)} %fusion.1293), channel_id=1, source_target_pairs={{1,0},{2,1},{3,2},{4,3},{5,4},{6,5},{7,6}} | collective-permute-start | bytes 1572872 | tf_op jit(solution)/shard_map/ppermute | solution.py:57
  795.0 11.4 %collective-permute-start.34 = (bf16[512,512]{1,0:T(8,128)(2,1)S(1)}, bf16[512,512]{1,0:T(8,128)(2,1)S(1)}, u32[]{:S(2)}, u32[]{:S(2)}) collective-permute-start(bf16[512,512]{1,0:T(8,128)(2,1)S(1)} %fusion.1292), channel_id=1, source_target_pairs={{1,0},{2,1},{3,2},{4,3},{5,4},{6,5},{7,6}} | collective-permute-start | bytes 1572872 | tf_op jit(solution)/shard_map/ppermute | solution.py:57
  821.5 11.4 %collective-permute-start.35 = (bf16[512,512]{1,0:T(8,128)(2,1)S(1)}, bf16[512,512]{1,0:T(8,128)(2,1)S(1)}, u32[]{:S(2)}, u32[]{:S(2)}) collective-permute-start(bf16[512,512]{1,0:T(8,128)(2,1)S(1)} %fusion.1291), channel_id=1, source_target_pairs={{1,0},{2,1},{3,2},{4,3},{5,4},{6,5},{7,6}} | collective-permute-start | bytes 1572872 | tf_op jit(solution)/shard_map/ppermute | solution.py:57
  848.0 11.4 %collective-permute-start.36 = (bf16[512,512]{1,0:T(8,128)(2,1)S(1)}, bf16[512,512]{1,0:T(8,128)(2,1)S(1)}, u32[]{:S(2)}, u32[]{:S(2)}) collective-permute-start(bf16[512,512]{1,0:T(8,128)(2,1)S(1)} %fusion.1290), channel_id=1, source_target_pairs={{1,0},{2,1},{3,2},{4,3},{5,4},{6,5},{7,6}} | collective-permute-start | bytes 1572872 | tf_op jit(solution)/shard_map/ppermute | solution.py:57
  874.5 11.4 %collective-permute-start.37 = (bf16[512,512]{1,0:T(8,128)(2,1)S(1)}, bf16[512,512]{1,0:T(8,128)(2,1)S(1)}, u32[]{:S(2)}, u32[]{:S(2)}) collective-permute-start(bf16[512,512]{1,0:T(8,128)(2,1)S(1)} %fusion.1289), channel_id=1, source_target_pairs={{1,0},{2,1},{3,2},{4,3},{5,4},{6,5},{7,6}} | collective-permute-start | bytes 1572872 | tf_op jit(solution)/shard_map/ppermute | solution.py:57
  901.0 11.4 %collective-permute-start.38 = (bf16[512,512]{1,0:T(8,128)(2,1)S(1)}, bf16[512,512]{1,0:T(8,128)(2,1)S(1)}, u32[]{:S(2)}, u32[]{:S(2)}) collective-permute-start(bf16[512,512]{1,0:T(8,128)(2,1)S(1)} %fusion.1288), channel_id=1, source_target_pairs={{1,0},{2,1},{3,2},{4,3},{5,4},{6,5},{7,6}} | collective-permute-start | bytes 1572872 | tf_op jit(solution)/shard_map/ppermute | solution.py:57
  927.5 11.4 %collective-permute-start.39 = (bf16[512,512]{1,0:T(8,128)(2,1)S(1)}, bf16[512,512]{1,0:T(8,128)(2,1)S(1)}, u32[]{:S(2)}, u32[]{:S(2)}) collective-permute-start(bf16[512,512]{1,0:T(8,128)(2,1)S(1)} %fusion.1287), channel_id=1, source_target_pairs={{1,0},{2,1},{3,2},{4,3},{5,4},{6,5},{7,6}} | collective-permute-start | bytes 1572872 | tf_op jit(solution)/shard_map/ppermute | solution.py:57
  954.0 11.4 %collective-permute-start.40 = (bf16[512,512]{1,0:T(8,128)(2,1)S(1)}, bf16[512,512]{1,0:T(8,128)(2,1)S(1)}, u32[]{:S(2)}, u32[]{:S(2)}) collective-permute-start(bf16[512,512]{1,0:T(8,128)(2,1)S(1)} %fusion.1286), channel_id=1, source_target_pairs={{1,0},{2,1},{3,2},{4,3},{5,4},{6,5},{7,6}} | collective-permute-start | bytes 1572872 | tf_op jit(solution)/shard_map/ppermute | solution.py:57
  980.5 11.4 %collective-permute-start.41 = (bf16[512,512]{1,0:T(8,128)(2,1)S(1)}, bf16[512,512]{1,0:T(8,128)(2,1)S(1)}, u32[]{:S(2)}, u32[]{:S(2)}) collective-permute-start(bf16[512,512]{1,0:T(8,128)(2,1)S(1)} %fusion.1285), channel_id=1, source_target_pairs={{1,0},{2,1},{3,2},{4,3},{5,4},{6,5},{7,6}} | collective-permute-start | bytes 1572872 | tf_op jit(solution)/shard_map/ppermute | solution.py:57
  1007.0 11.4 %collective-permute-start.42 = (bf16[512,512]{1,0:T(8,128)(2,1)S(1)}, bf16[512,512]{1,0:T(8,128)(2,1)S(1)}, u32[]{:S(2)}, u32[]{:S(2)}) collective-permute-start(bf16[512,512]{1,0:T(8,128)(2,1)S(1)} %fusion.1284), channel_id=1, source_target_pairs={{1,0},{2,1},{3,2},{4,3},{5,4},{6,5},{7,6}} | collective-permute-start | bytes 1572872 | tf_op jit(solution)/shard_map/ppermute | solution.py:57
  1033.5 11.4 %collective-permute-start.43 = (bf16[512,512]{1,0:T(8,128)(2,1)S(1)}, bf16[512,512]{1,0:T(8,128)(2,1)S(1)}, u32[]{:S(2)}, u32[]{:S(2)}) collective-permute-start(bf16[512,512]{1,0:T(8,128)(2,1)S(1)} %fusion.1283), channel_id=1, source_target_pairs={{1,0},{2,1},{3,2},{4,3},{5,4},{6,5},{7,6}} | collective-permute-start | bytes 1572872 | tf_op jit(solution)/shard_map/ppermute | solution.py:57
  (52 other events, 253.5 us)
where the time goes:
time: 1090 us; the launch traced here: 1080 us
  matrix products  548 us (50%)
  waiting for transfers between devices  210 us (19%)
  starting transfers between devices  162 us (15%)
  other arithmetic  97.5 us (9%)
  local copies, waits for them, and re-layouts  54.9 us (5%)
    dot_general x90, matrix products, layer(): gate = jnp.dot(a, w['w_gate'], preferred_element_type=jnp.float32)  224 us
    dot_general x68, matrix products, matmul(): jnp.dot(a, w, preferred_element_type=jnp.float32).astype(jnp.bfloat16)  203 us
    ppermute x22, waiting for transfers between devices, step(): came = lax.ppermute(by_h, 'pp', back_again)  146 us
    dot_general x68, matrix products, layer(): up = jnp.dot(a, w['w_up'], preferred_element_type=jnp.float32)  120 us
    ppermute x22, starting transfers between devices, step(): came = lax.ppermute(stage(weights, h), 'pp', onward)  114 us
    ppermute x22, waiting for transfers between devices, step(): came = lax.ppermute(stage(weights, h), 'pp', onward)  64.5 us
    ppermute x22, starting transfers between devices, step(): came = lax.ppermute(by_h, 'pp', back_again)  48.1 us
    dynamic_update_slice x23, other arithmetic, step(): lax.dynamic_update_index_in_dim(kept, jnp.where(at_work, h, was), number, 0)  34.3 us
  transfers between devices with their start and end apart: 44, of which 41 were waited for; matrix products, arithmetic and copies ran while one was open for 12% of the time, Pallas kernels for 0%

commit v1 on v0

v1 whole, which is shorter than its diff:
```python
import functools

import jax
import jax.numpy as jnp
from jax import lax
from jax.experimental import pallas as pl
from jax.experimental.pallas import tpu as pltpu
from jax.sharding import PartitionSpec as P

f32, bf16 = jnp.float32, jnp.bfloat16
MESH = pl.DeviceIdType.MESH
ROWS = 256
BLOCK = 256
RING = 8
LEAD = (16, 14, 11, 10, 7, 5, 2, 0)
VMEM_BYTES = 64 * 2**20 - 2**16


def mm(a, b):
    return jnp.dot(a, b, preferred_element_type=f32)


def mm_nt(a, b):
    return lax.dot_general(a, b, (((1,), (1,)), ((), ())), preferred_element_type=f32)


def mm_tn(a, b):
    return lax.dot_general(a, b, (((0,), (0,)), ((), ())), preferred_element_type=f32)


def norm_of(h):
    wide = h.astype(f32)
    return wide, lax.rsqrt(jnp.mean(wide * wide, -1, keepdims=True) + 1e-6)


def blocks(ff):
    return [slice(at, at + BLOCK) for at in range(0, ff, BLOCK)]


def forward(h, wg, wu, wd, hidden):
    wide, scale = norm_of(h)
    a = (wide * scale).astype(bf16)
    for c in blocks(hidden.shape[1]):
        gate, up = mm(a, wg[:, c]), mm(a, wu[:, c])
        hidden[:, c] = (gate * jax.nn.sigmoid(gate) * up).astype(bf16)
    return h + mm(hidden[...], wd[...]).astype(bf16)


def backward(h, by_y, wg, wu, wd, a_all, hid_all, by_gate, by_up, rows):
    wide, scale = norm_of(h)
    a = (wide * scale).astype(bf16)
    a_all[rows, :] = a
    for c in blocks(hid_all.shape[1]):
        gate, up = mm(a, wg[:, c]), mm(a, wu[:, c])
        by_hid = mm_nt(by_y, wd[c, :]).astype(bf16).astype(f32)
        sig = jax.nn.sigmoid(gate)
        silu = gate * sig
        hid_all[rows, c] = (silu * up).astype(bf16)
        by_up[rows, c] = (by_hid * silu).astype(bf16)
        by_gate[rows, c] = ((by_hid * up) * (sig + silu * (1.0 - sig))).astype(bf16)
    return wide, scale


def backward_input(wide, scale, by_y, wg, wu, by_gate, by_up, rows):
    by_a = mm_nt(by_gate[rows, :], wg[...]).astype(bf16) + mm_nt(by_up[rows, :], wu[...]).astype(bf16)
    by_a = by_a.astype(f32)
    inner = jnp.sum(by_a * wide, -1, keepdims=True) * (1.0 / wide.shape[1])
    return by_y + (by_a * scale - wide * (scale * scale * scale * inner)).astype(bf16)


def kernel(stages, chunks, per, x, dy, wg, wu, wd, o_gate, o_up, o_down, kept, came, f_out, b_out, hidden, a_all, hid_all, by_gate, by_up,
           acc, f_in, b_in, f_sent, b_sent):
    me = lax.axis_index("pp")
    first, last = me == 0, me == stages - 1
    lead = sum(jnp.where(me == i, n, 0) for i, n in enumerate(LEAD))
    ff = hidden.shape[1]

    barrier = pltpu.get_barrier_semaphore()

    @pl.when(jnp.logical_not(last))
    def _():
        pl.semaphore_signal(barrier, inc=1, device_id={"pp": me + 1}, device_id_type=MESH)

    @pl.when(jnp.logical_not(first))
    def _():
        pl.semaphore_signal(barrier, inc=1, device_id={"pp": me - 1}, device_id_type=MESH)

    pl.semaphore_wait(barrier, jnp.where(first | last, 1, 2))

    def load(source, target, sems):
        def one(k, _):
            pltpu.make_async_copy(source.at[k], target.at[k], sems.at[k]).start()
            return 0

        lax.fori_loop(0, chunks, one, 0)

    @pl.when(first)
    def _():
        load(x, kept, f_in)

    @pl.when(last)
    def _():
        load(dy, came, b_in)

    acc[...] = jnp.zeros_like(acc)

    def send(k, out, into, sent, arrived, to):
        slot = lax.rem(k, RING)
        return pltpu.make_async_remote_copy(
            src_ref=out.at[slot], dst_ref=into.at[k], send_sem=sent.at[slot], recv_sem=arrived.at[k], device_id={"pp": to}, device_id_type=MESH
        )

    def f_send(k):
        return send(k, f_out, kept, f_sent, f_in, me + 1)

    def b_send(k):
        return send(k, b_out, came, b_sent, b_in, me - 1)

    def arrived(k, into, sems):
        pltpu.make_async_copy(into.at[k], into.at[k], sems.at[k]).wait()

    def take(t, _):
        k = t

        @pl.when(k < chunks)
        def _():
            arrived(k, kept, f_in)

        @pl.when((k < chunks) & jnp.logical_not(last))
        def _():
            @pl.when(k >= RING)
            def _():
                f_send(k - RING).wait_send()

            f_out[lax.rem(k, RING)] = forward(kept[k], wg, wu, wd, hidden)
            f_send(k).start()

        j = t - lead

        @pl.when((j >= 0) & (j < chunks))
        def _():
            arrived(j, came, b_in)
            rows = pl.ds(pl.multiple_of(lax.rem(j, per) * ROWS, ROWS), ROWS)
            by_y = came[j]
            wide, scale = backward(kept[j], by_y, wg, wu, wd, a_all, hid_all, by_gate, by_up, rows)

            @pl.when(jnp.logical_not(first))
            def _():
                @pl.when(j >= RING)
                def _():
                    b_send(j - RING).wait_send()

                b_out[lax.rem(j, RING)] = backward_input(*norm_of(kept[j]), came[j], wg, wu, by_gate, by_up, rows)
                b_send(j).start()

            @pl.when(lax.rem(j, per) == per - 1)
            def _():
                for c in blocks(ff):
                    by_out = jnp.concatenate([came[j - per + 1 + i] for i in range(per)], axis=0)
                    acc[0, :, c] += mm_tn(a_all[...], by_gate[:, c]).astype(bf16).astype(f32)
                    acc[1, :, c] += mm_tn(a_all[...], by_up[:, c]).astype(bf16).astype(f32)
                    acc[2, :, c] += mm_tn(by_out, hid_all[:, c]).astype(bf16).astype(f32)

        return 0

    lax.fori_loop(0, chunks + lead, take, 0)

    def drain(i, _):
        @pl.when(jnp.logical_not(last))
        def _():
            f_send(chunks - RING + i).wait_send()

        @pl.when(jnp.logical_not(first))
        def _():
            b_send(chunks - RING + i).wait_send()

        return 0

    lax.fori_loop(0, RING, drain, 0)
    o_gate[...] = acc[0].astype(bf16)
    o_up[...] = acc[1].astype(bf16)
    o_down[...] = acc[2].astype(bf16)


def solution(mesh):
    stages = mesh.shape["pp"]

    def step(x, dy, w_gate, w_up, w_down):
        micro, tokens, d = x.shape
        ff = w_gate.shape[2]
        per = tokens // ROWS
        chunks = micro * per
        x, dy = (v.reshape(chunks, ROWS, d) for v in (x, dy))
        vmem, anywhere = pl.BlockSpec(memory_space=pltpu.VMEM), pl.BlockSpec(memory_space=pl.ANY)
        by_gate, by_up, by_down = pl.pallas_call(
            functools.partial(kernel, stages, chunks, per),
            out_shape=[jax.ShapeDtypeStruct((d, ff), bf16)] * 3,
            in_specs=[anywhere] * 2 + [vmem] * 3,
            out_specs=[vmem] * 3,
            scratch_shapes=[
                pltpu.VMEM((chunks, ROWS, d), bf16),
                pltpu.VMEM((chunks, ROWS, d), bf16),
                pltpu.VMEM((RING, ROWS, d), bf16),
                pltpu.VMEM((RING, ROWS, d), bf16),
                pltpu.VMEM((ROWS, ff), bf16),
                pltpu.VMEM((tokens, d), bf16),
                pltpu.VMEM((tokens, ff), bf16),
                pltpu.VMEM((tokens, ff), bf16),
                pltpu.VMEM((tokens, ff), bf16),
                pltpu.VMEM((3, d, ff), f32),
                pltpu.SemaphoreType.DMA((chunks,)),
                pltpu.SemaphoreType.DMA((chunks,)),
                pltpu.SemaphoreType.DMA((RING,)),
                pltpu.SemaphoreType.DMA((RING,)),
            ],
            compiler_params=pltpu.CompilerParams(collective_id=0, has_side_effects=True, vmem_limit_bytes=VMEM_BYTES),
            cost_estimate=pl.CostEstimate(flops=22 * micro * tokens * d * ff, bytes_accessed=16 * d * ff, transcendentals=0),
        )(x, dy, w_gate[0], w_up[0], w_down[0])
        return by_gate[None], by_up[None], by_down.T[None]

    return jax.shard_map(
        step,
        mesh=mesh,
        in_specs=(P("rep", None, None),) * 2 + (P("pp", None, None),) * 3,
        out_specs=(P(("rep", "pp"), None, None),) * 3,
        check_vma=False,
    )
```

time: 1090 us -> 256 us (0.23)
  the two profiles are of different devices: /device:TPU:5 before, /device:TPU:0 now
where the time goes in v1:
time: 256 us
  Pallas kernels  250 us (98%)
  local copies, waits for them, and re-layouts  5.38 us (2%)
    pallas_call x1, Pallas kernels, step(): pl.pallas_call(functools.partial(kernel, stages, chunks, per), out_shape=...  250 us
    unnamed x7, local copies, waits for them, and re-layouts  5.38 us

profile of v1, /device:TPU:0, one launch (start us, length us, event | category | flops | bytes accessed | tf_op | source)
XLA Modules:
  0.0 255.9 jit_solution(15840948419897746949)
XLA Ops:
  0.6 249.8 %shard_map.76 = (bf16[512,1280]{1,0:T(8,128)(2,1)}, bf16[512,1280]{1,0:T(8,128)(2,1)}, bf16[512,1280]{1,0:T(8,128)(2,1)}) custom-call(bf16[32,256,512]{2,1,0:T(8,128)(2,1)} %bitcast.13, bf16[32,256,512]{2,1,0:T(8,128)(2,1)} %bitcast.14, bf16[512,1280]{1,0:T(8,128)(2,1)} %bitcast.15, bf16[512,1280]{1,0:T(8,128)(2,1)} %bitcast.16, bf16[1280,512]{1,0:T(8,128)(2,1)} %bitcast.17), custom_call_target="tpu_custom_call" | custom-call | flops 118111600640 | bytes 10485760 | tf_op jit(solution)/shard_map/pallas_call | solution.py:195
  250.5 0.0 copy-start.1
  250.5 2.5 copy.8
  253.0 0.0 copy-done.1
  253.0 0.0 copy-start
  253.0 1.1 copy.11
  254.1 0.7 copy-done
  254.8 1.1 copy.12
Async XLA Ops:
  250.5 2.5 copy-start.1
  253.0 1.8 copy-start

commit v2 on v1

v2 whole, which is shorter than its diff:
```python
import functools

import jax
import jax.numpy as jnp
from jax import lax
from jax.experimental import pallas as pl
from jax.experimental.pallas import tpu as pltpu
from jax.sharding import PartitionSpec as P

f32, bf16 = jnp.float32, jnp.bfloat16
MESH = pl.DeviceIdType.MESH
ROWS = 256
BLOCK = 256
RING = 4
LEAD = (28, 24, 15, 13, 8, 6, 2, 0)
CROSS = 3
F_RELAY, B_RELAY = 0, 7
F_FAR, B_FAR = 144, 112
F_SPLIT, B_SPLIT = (7, 31), (0, 20)
F_BEHIND, B_BEHIND = 10, 6
MERGED = ()
STASHED, SLOTS = (4, 5, 6), 9
VMEM_BYTES = 60 * 2**20


def mm(a, b):
    return jnp.dot(a, b, preferred_element_type=f32)


def mm_nt(a, b):
    return lax.dot_general(a, b, (((1,), (1,)), ((), ())), preferred_element_type=f32)


def mm_tn(a, b):
    return lax.dot_general(a, b, (((0,), (0,)), ((), ())), preferred_element_type=f32)


def norm_of(h):
    wide = h.astype(f32)
    return wide, lax.rsqrt(jnp.mean(wide * wide, -1, keepdims=True) + 1e-6)


def blocks(ff):
    return [slice(at, at + BLOCK) for at in range(0, ff, BLOCK)]


def forward(h, wg, wu, wd, hidden, stash=None):
    wide, scale = norm_of(h)
    a = (wide * scale).astype(bf16)
    for c in blocks(hidden.shape[1]):
        gate, up = mm(a, wg[:, c]), mm(a, wu[:, c])
        if stash is not None:
            stash[0, :, c], stash[1, :, c] = gate, up
        hidden[:, c] = (gate * jax.nn.sigmoid(gate) * up).astype(bf16)
    return h + mm(hidden[...], wd[...]).astype(bf16)


def backward(h, by_y, wg, wu, wd, a_all, hid_all, by_gate, by_up, rows, stash=None):
    wide, scale = norm_of(h)
    a = (wide * scale).astype(bf16)
    a_all[rows, :] = a
    for c in blocks(hid_all.shape[1]):
        gate, up = (mm(a, wg[:, c]), mm(a, wu[:, c])) if stash is None else (stash[0, :, c], stash[1, :, c])
        by_hid = mm_nt(by_y, wd[c, :]).astype(bf16).astype(f32)
        sig = jax.nn.sigmoid(gate)
        silu = gate * sig
        hid_all[rows, c] = (silu * up).astype(bf16)
        by_up[rows, c] = (by_hid * silu).astype(bf16)
        by_gate[rows, c] = ((by_hid * up) * (sig + silu * (1.0 - sig))).astype(bf16)
    return wide, scale


def backward_input(wide, scale, by_y, wg, wu, by_gate, by_up, rows):
    by_a = mm_nt(by_gate[rows, :], wg[...]).astype(bf16) + mm_nt(by_up[rows, :], wu[...]).astype(bf16)
    by_a = by_a.astype(f32)
    inner = jnp.sum(by_a * wide, -1, keepdims=True) * (1.0 / wide.shape[1])
    return by_y + (by_a * scale - wide * (scale * scale * scale * inner)).astype(bf16)


def kernel(stages, chunks, per, x, dy, wg, wu, wd, o_gate, o_up, o_down, kept, came, f_out, b_out, hidden, a_all, hid_all,
           acc, acc_down, relay, stash, f_in, b_in, f_sent, b_sent, f_round, b_round, r_in, r_sent, x_sent):
    me = lax.axis_index("pp")
    first, last = me == 0, me == stages - 1
    lead = sum(jnp.where(me == i, n, 0) for i, n in enumerate(LEAD))
    ff = hidden.shape[1]
    by_gate, by_up = o_gate, o_up

    barrier = pltpu.get_barrier_semaphore()

    @pl.when(jnp.logical_not(last))
    def _():
        pl.semaphore_signal(barrier, inc=1, device_id={"pp": me + 1}, device_id_type=MESH)

    @pl.when(jnp.logical_not(first))
    def _():
        pl.semaphore_signal(barrier, inc=1, device_id={"pp": me - 1}, device_id_type=MESH)

    pairs = [(CROSS, F_RELAY), (F_RELAY, CROSS + 1), (CROSS + 1, B_RELAY), (B_RELAY, CROSS)]
    for one, other in pairs + [(b, a) for a, b in pairs]:

        @pl.when(me == one)
        def _():
            pl.semaphore_signal(barrier, inc=1, device_id={"pp": other}, device_id_type=MESH)

    greeted = jnp.where(first | last, 1, 2) + sum(jnp.where(me == one, 1, 0) for pair in pairs for one in pair)
    pl.semaphore_wait(barrier, greeted)

    def load(source, target, sems):
        def one(k, _):
            pltpu.make_async_copy(source.at[k], target.at[k], sems.at[k]).start()
            return 0

        lax.fori_loop(0, chunks, one, 0)

    @pl.when(first)
    def _():
        load(x, kept, f_in)

    @pl.when(last)
    def _():
        load(dy, came, b_in)

    acc[...] = jnp.zeros_like(acc)
    acc_down[...] = jnp.zeros_like(acc_down)

    def send(k, out, into, sent, arrived, to):
        slot = lax.rem(k, RING)
        return pltpu.make_async_remote_copy(
            src_ref=out.at[slot], dst_ref=into.at[k], send_sem=sent.at[slot], recv_sem=arrived.at[k], device_id={"pp": to}, device_id_type=MESH
        )

    def f_split(k):
        return (k >= F_SPLIT[0]) & (k < F_SPLIT[1])

    def b_split(k):
        return (k >= B_SPLIT[0]) & (k < B_SPLIT[1])

    f_cut, b_cut = ((pl.ds(0, ROWS - far), pl.ds(ROWS - far, far), pl.ds(0, far), span[0]) for far, span in ((F_FAR, F_SPLIT), (B_FAR, B_SPLIT)))

    def halves(k, out, into, sent, arrived, to, by, cut):
        slot = lax.rem(k, RING)
        near, far, at, base = cut
        return (
            pltpu.make_async_remote_copy(
                src_ref=out.at[slot, near], dst_ref=into.at[k, near], send_sem=sent.at[slot], recv_sem=arrived.at[k], device_id={"pp": to},
                device_id_type=MESH,
            ),
            pltpu.make_async_remote_copy(
                src_ref=out.at[slot, far], dst_ref=relay.at[k - base, at], send_sem=x_sent.at[slot], recv_sem=r_in.at[k], device_id={"pp": by},
                device_id_type=MESH,
            ),
        )

    def pass_on(k, into, round_, to, cut):
        return pltpu.make_async_remote_copy(
            src_ref=relay.at[k - cut[3], cut[2]], dst_ref=into.at[k, cut[1]], send_sem=r_sent.at[k], recv_sem=round_.at[k], device_id={"pp": to},
            device_id_type=MESH,
        )

    f_pass = lambda k: pass_on(k, kept, f_round, CROSS + 1, f_cut)
    b_pass = lambda k: pass_on(k, came, b_round, CROSS, b_cut)

    def either(split, whole, parts):
        @pl.when(jnp.logical_not(split))
        def _():
            whole()

        @pl.when(split)
        def _():
            parts()

    def f_do(k, what):
        def parts():
            for copy in halves(k, f_out, kept, f_sent, f_in, CROSS + 1, F_RELAY, f_cut):
                what(copy)

        either((me == CROSS) & f_split(k), lambda: what(send(k, f_out, kept, f_sent, f_in, me + 1)), parts)

    def b_do(k, what):
        def parts():
            for copy in halves(k, b_out, came, b_sent, b_in, CROSS, B_RELAY, b_cut):
                what(copy)

        either((me == CROSS + 1) & b_split(k), lambda: what(send(k, b_out, came, b_sent, b_in, me - 1)), parts)

    start, wait_send = lambda copy: copy.start(), lambda copy: copy.wait_send()

    def arrived(k, into, sems, round_, split, cut):
        def parts():
            for rows, sem in zip(cut, (sems, round_)):
                pltpu.make_async_copy(into.at[k, rows], into.at[k, rows], sem.at[k]).wait()

        either(split, lambda: pltpu.make_async_copy(into.at[k], into.at[k], sems.at[k]).wait(), parts)

    stashes = sum(jnp.where(me == i, 1, 0) for i in STASHED) > 0

    merges = sum([jnp.where(me == i, 1, 0) for i in MERGED], 0) > 0
    middle = jnp.logical_not(first | stashes)

    def take(t, _):
        for by, behind, split, copy, cut in ((F_RELAY, F_BEHIND, f_split, f_pass, f_cut), (B_RELAY, B_BEHIND, b_split, b_pass, b_cut)):

            @pl.when((me == by) & (t >= behind) & split(t - behind))
            def _():
                here = relay.at[t - behind - cut[3], cut[2]]
                pltpu.make_async_copy(here, here, r_in.at[t - behind]).wait()
                copy(t - behind).start()

        k, j = t, t - lead
        has_f, has_b = (k < chunks) & jnp.logical_not(last), (j >= 0) & (j < chunks)
        rows = pl.ds(pl.multiple_of(lax.rem(j + chunks, per) * ROWS, ROWS), ROWS)
        out = jnp.logical_not(first)

        @pl.when(k < chunks)
        def _():
            arrived(k, kept, f_in, f_round, (me == CROSS + 1) & f_split(k), f_cut)

        @pl.when(has_f & (k >= RING))
        def _():
            f_do(k - RING, wait_send)

        def await_b():
            arrived(j, came, b_in, b_round, (me == CROSS) & b_split(j), b_cut)

            @pl.when(out & (j >= RING))
            def _():
                b_do(j - RING, wait_send)

        def work(forth, back, whole=True, stashed=False):
            if back:
                kept_of = stash.at[lax.rem(j, SLOTS)] if stashed else None
                wide, scale = backward(kept[j], came[j], wg, wu, wd, a_all, hid_all, by_gate, by_up, rows, kept_of)
                if whole:
                    b_out[lax.rem(j, RING)] = backward_input(wide, scale, came[j], wg, wu, by_gate, by_up, rows)
            if forth:
                f_out[lax.rem(k, RING)] = forward(kept[k], wg, wu, wd, hidden, stash.at[lax.rem(k, SLOTS)] if stashed else None)

        joint = has_f & has_b & merges
        if set(MERGED):
            pl.when(joint)(await_b)
            if 0 in MERGED:
                pl.when(joint & first)(lambda: work(True, True, whole=False))
            if set(MERGED) - set(STASHED) - {0}:
                pl.when(joint & middle)(lambda: work(True, True))
            if set(MERGED) & set(STASHED):
                pl.when(joint & stashes)(lambda: work(True, True, stashed=True))

        pl.when(has_f & jnp.logical_not(joint))(lambda: work(True, False, stashed=True))

        @pl.when(has_f)
        def _():
            f_do(k, start)

        only_b = has_b & jnp.logical_not(joint)
        pl.when(only_b)(await_b)
        pl.when(only_b & first)(lambda: work(False, True, whole=False))
        pl.when(only_b & middle)(lambda: work(False, True))
        pl.when(only_b & stashes)(lambda: work(False, True, stashed=True))

        @pl.when(has_b & out)
        def _():
            b_do(j, start)

        @pl.when(has_b & (lax.rem(j + chunks, per) == per - 1))
        def _():
            by_out = jnp.concatenate([came[j - per + 1 + i] for i in range(per)], axis=0)
            for c in blocks(ff):
                acc[0, :, c] += mm_tn(a_all[...], by_gate[:, c]).astype(bf16).astype(f32)
                acc[1, :, c] += mm_tn(a_all[...], by_up[:, c]).astype(bf16).astype(f32)
                acc_down[c, :] += mm_tn(hid_all[:, c], by_out).astype(bf16).astype(f32)

        return 0

    steps = chunks + jnp.maximum(lead, jnp.where(me == F_RELAY, F_BEHIND, jnp.where(me == B_RELAY, B_BEHIND, 0)))
    lax.fori_loop(0, steps, take, 0)

    def drain(i, _):
        @pl.when(jnp.logical_not(last))
        def _():
            f_do(chunks - RING + i, wait_send)

        @pl.when(jnp.logical_not(first))
        def _():
            b_do(chunks - RING + i, wait_send)

        return 0

    lax.fori_loop(0, RING, drain, 0)
    for by, span, copy in ((F_RELAY, F_SPLIT, f_pass), (B_RELAY, B_SPLIT, b_pass)):

        @pl.when(me == by)
        def _():
            def passed(k, _):
                copy(k).wait_send()
                return 0

            lax.fori_loop(*span, passed, 0)

    o_gate[...] = acc[0].astype(bf16)
    o_up[...] = acc[1].astype(bf16)
    o_down[...] = acc_down[...].astype(bf16)


def write_out(*refs):
    sources, targets, sems = refs[:3], refs[3:6], refs[6]
    copies = [pltpu.make_async_copy(source, target, sems.at[i]) for i, (source, target) in enumerate(zip(sources, targets))]
    for copy in copies:
        copy.start()
    for copy in copies:
        copy.wait()


def solution(mesh):
    stages = mesh.shape["pp"]

    def step(x, dy, w_gate, w_up, w_down):
        micro, tokens, d = x.shape
        ff = w_gate.shape[2]
        per = tokens // ROWS
        chunks = micro * per
        x, dy = (v.reshape(chunks, ROWS, d) for v in (x, dy))
        vmem, anywhere = pl.BlockSpec(memory_space=pltpu.VMEM), pl.BlockSpec(memory_space=pl.ANY)
        by_gate, by_up, by_down = pl.pallas_call(
            functools.partial(kernel, stages, chunks, per),
            out_shape=[pltpu.VMEM((d, ff), bf16)] * 2 + [pltpu.VMEM((ff, d), bf16)],
            in_specs=[anywhere] * 2 + [vmem] * 3,
            out_specs=[vmem] * 3,
            scratch_shapes=[
                pltpu.VMEM((chunks, ROWS, d), bf16),
                pltpu.VMEM((chunks, ROWS, d), bf16),
                pltpu.VMEM((RING, ROWS, d), bf16),
                pltpu.VMEM((RING, ROWS, d), bf16),
                pltpu.VMEM((ROWS, ff), bf16),
                pltpu.VMEM((tokens, d), bf16),
                pltpu.VMEM((tokens, ff), bf16),
                pltpu.VMEM((2, d, ff), f32),
                pltpu.VMEM((ff, d), f32),
                pltpu.VMEM((max(b - a for a, b in (F_SPLIT, B_SPLIT)), max(F_FAR, B_FAR), d), bf16),
                pltpu.VMEM((SLOTS, 2, ROWS, ff), f32),
                pltpu.SemaphoreType.DMA((chunks,)),
                pltpu.SemaphoreType.DMA((chunks,)),
                pltpu.SemaphoreType.DMA((RING,)),
                pltpu.SemaphoreType.DMA((RING,)),
                pltpu.SemaphoreType.DMA((chunks,)),
                pltpu.SemaphoreType.DMA((chunks,)),
                pltpu.SemaphoreType.DMA((chunks,)),
                pltpu.SemaphoreType.DMA((chunks,)),
                pltpu.SemaphoreType.DMA((RING,)),
            ],
            compiler_params=pltpu.CompilerParams(collective_id=0, has_side_effects=True, vmem_limit_bytes=VMEM_BYTES),
            cost_estimate=pl.CostEstimate(flops=22 * micro * tokens * d * ff, bytes_accessed=16 * d * ff, transcendentals=0),
        )(x, dy, w_gate[0], w_up[0], w_down[0])
        outs = pl.pallas_call(
            write_out,
            out_shape=[jax.ShapeDtypeStruct(v.shape, bf16) for v in (by_gate, by_up, by_down)],
            in_specs=[vmem] * 3,
            out_specs=[anywhere] * 3,
            scratch_shapes=[pltpu.SemaphoreType.DMA((3,))],
            compiler_params=pltpu.CompilerParams(vmem_limit_bytes=2**20),
        )(by_gate, by_up, by_down)
        return tuple(v[None] for v in outs)

    return jax.shard_map(
        step,
        mesh=mesh,
        in_specs=(P("rep", None, None),) * 2 + (P("pp", None, None),) * 3,
        out_specs=(P(("rep", "pp"), None, None),) * 3,
        check_vma=False,
    )
```

time: 256 us -> 212 us (0.83)
  Pallas kernels: 250 us -> 211 us
  local copies, waits for them, and re-layouts: 5.38 us -> 0 us
    pallas_call x1, Pallas kernels: 250 us -> 209 us  [step(): pl.pallas_call(functools.partial(kernel, stages, chunks, per), out_shape=...]
    unnamed x7 -> x0, local copies, waits for them, and re-layouts: 5.38 us -> none
where the time goes in v2:
time: 212 us
  Pallas kernels  211 us (100%)
    pallas_call x1, Pallas kernels, step(): pl.pallas_call(functools.partial(kernel, stages, chunks, per), out_shape=...  209 us

profile of v2, /device:TPU:0, one launch (start us, length us, event | category | flops | bytes accessed | tf_op | source)
XLA Modules:
  0.0 212.0 jit_solution(12872131976758572065)
XLA Ops:
  0.6 209.4 %shard_map.76 = (bf16[512,1280]{1,0:T(8,128)(2,1)S(1)}, bf16[512,1280]{1,0:T(8,128)(2,1)S(1)}, bf16[1280,512]{1,0:T(8,128)(2,1)S(1)}) custom-call(bf16[32,256,512]{2,1,0:T(8,128)(2,1)} %bitcast.8, bf16[32,256,512]{2,1,0:T(8,128)(2,1)} %bitcast.9, bf16[512,1280]{1,0:T(8,128)(2,1)} %bitcast.10, bf16[512,1280]{1,0:T(8,128)(2,1)} %bitcast.11, ...), custom_call_target="tpu_custom_call" | custom-call | flops 118111600640 | bytes 10485760 | tf_op jit(solution)/shard_map/pallas_call | solution.py:323
  210.1 1.9 shard_map.77

commit v3 on v2

--- a/solution.py
+++ b/solution.py
@@ -18,8 +18,9 @@
 F_FAR, B_FAR = 144, 112
 F_SPLIT, B_SPLIT = (7, 31), (0, 20)
 F_BEHIND, B_BEHIND = 10, 6
-MERGED = ()
-STASHED, SLOTS = (4, 5, 6), 9
+COVERED = ()
+STASHED, SLOTS = (1, 2, 3, 4, 5, 6), 9
+AWAY, OUTGOING, INCOMING, SOON = (1, 2, 3), 4, 4, 3
 VMEM_BYTES = 60 * 2**20
 
 
@@ -77,8 +78,8 @@
     return by_y + (by_a * scale - wide * (scale * scale * scale * inner)).astype(bf16)
 
 
-def kernel(stages, chunks, per, x, dy, wg, wu, wd, o_gate, o_up, o_down, kept, came, f_out, b_out, hidden, a_all, hid_all,
-           acc, acc_down, relay, stash, f_in, b_in, f_sent, b_sent, f_round, b_round, r_in, r_sent, x_sent):
+def kernel(stages, chunks, per, x, dy, wg, wu, wd, o_gate, o_up, o_down, store, kept, came, f_out, b_out, hidden, a_all, hid_all,
+           acc, acc_down, relay, stash, f_in, b_in, f_sent, b_sent, f_round, b_round, r_in, r_sent, x_sent, s_out, s_back):
     me = lax.axis_index("pp")
     first, last = me == 0, me == stages - 1
     lead = sum(jnp.where(me == i, n, 0) for i, n in enumerate(LEAD))
@@ -194,7 +195,8 @@
 
     stashes = sum(jnp.where(me == i, 1, 0) for i in STASHED) > 0
 
-    merges = sum([jnp.where(me == i, 1, 0) for i in MERGED], 0) > 0
+    away = sum([jnp.where(me == i, 1, 0) for i in AWAY], 0) > 0
+    covers = sum([jnp.where(me == i, 1, 0) for i in COVERED], 0) > 0
     middle = jnp.logical_not(first | stashes)
 
     def take(t, _):
@@ -211,6 +213,36 @@
         rows = pl.ds(pl.multiple_of(lax.rem(j + chunks, per) * ROWS, ROWS), ROWS)
         out = jnp.logical_not(first)
 
+        def weights():
+            by_out = jnp.concatenate([came[j - per + i] for i in range(per)], axis=0)
+            for c in blocks(ff):
+                acc[0, :, c] += mm_tn(a_all[...], by_gate[:, c]).astype(bf16).astype(f32)
+                acc[1, :, c] += mm_tn(a_all[...], by_up[:, c]).astype(bf16).astype(f32)
+                acc_down[c, :] += mm_tn(hid_all[:, c], by_out).astype(bf16).astype(f32)
+
+        due = (j >= per) & (j <= chunks) & (lax.rem(j + chunks, per) == 0)
+        f_slot = jnp.where(away, lax.rem(k, OUTGOING), lax.rem(k, SLOTS))
+        b_slot = jnp.where(away, OUTGOING + lax.rem(j + chunks, INCOMING), lax.rem(j + SLOTS * chunks, SLOTS))
+
+        def put(k):
+            slot = lax.rem(k, OUTGOING)
+            return pltpu.make_async_copy(stash.at[slot], store.at[k], s_out.at[slot])
+
+        def get(j):
+            slot = lax.rem(j, INCOMING)
+            return pltpu.make_async_copy(store.at[j], stash.at[OUTGOING + slot], s_back.at[slot])
+
+        @pl.when(away & (k >= OUTGOING) & (k < chunks + OUTGOING))
+        def _():
+            put(k - OUTGOING).wait()
+
+        @pl.when(away & (j + SOON >= 0) & (j + SOON < chunks))
+        def _():
+            get(j + SOON).start()
+
+        covered = due & has_f & covers
+        pl.when(due & jnp.logical_not(covered))(weights)
+
         @pl.when(k < chunks)
         def _():
             arrived(k, kept, f_in, f_round, (me == CROSS + 1) & f_split(k), f_cut)
@@ -226,52 +258,46 @@
             def _():
                 b_do(j - RING, wait_send)
 
+            @pl.when(away)
+            def _():
+                get(j).wait()
+
         def work(forth, back, whole=True, stashed=False):
             if back:
-                kept_of = stash.at[lax.rem(j, SLOTS)] if stashed else None
+                kept_of = stash.at[b_slot] if stashed else None
                 wide, scale = backward(kept[j], came[j], wg, wu, wd, a_all, hid_all, by_gate, by_up, rows, kept_of)
                 if whole:
                     b_out[lax.rem(j, RING)] = backward_input(wide, scale, came[j], wg, wu, by_gate, by_up, rows)
             if forth:
-                f_out[lax.rem(k, RING)] = forward(kept[k], wg, wu, wd, hidden, stash.at[lax.rem(k, SLOTS)] if stashed else None)
-
-        joint = has_f & has_b & merges
-        if set(MERGED):
-            pl.when(joint)(await_b)
-            if 0 in MERGED:
-                pl.when(joint & first)(lambda: work(True, True, whole=False))
-            if set(MERGED) - set(STASHED) - {0}:
-                pl.when(joint & middle)(lambda: work(True, True))
-            if set(MERGED) & set(STASHED):
-                pl.when(joint & stashes)(lambda: work(True, True, stashed=True))
-
-        pl.when(has_f & jnp.logical_not(joint))(lambda: work(True, False, stashed=True))
+                f_out[lax.rem(k, RING)] = forward(kept[k], wg, wu, wd, hidden, stash.at[f_slot] if stashed else None)
+
+        @pl.when(covered)
+        def _():
+            weights()
+            work(True, False, stashed=True)
+
+        pl.when(has_f & jnp.logical_not(covered))(lambda: work(True, False, stashed=True))
 
         @pl.when(has_f)
         def _():
             f_do(k, start)
 
-        only_b = has_b & jnp.logical_not(joint)
-        pl.when(only_b)(await_b)
-        pl.when(only_b & first)(lambda: work(False, True, whole=False))
-        pl.when(only_b & middle)(lambda: work(False, True))
-        pl.when(only_b & stashes)(lambda: work(False, True, stashed=True))
+        @pl.when(has_f & away)
+        def _():
+            put(k).start()
+
+        pl.when(has_b)(await_b)
+        pl.when(has_b & first)(lambda: work(False, True, whole=False))
+        pl.when(has_b & middle)(lambda: work(False, True))
+        pl.when(has_b & stashes)(lambda: work(False, True, stashed=True))
 
         @pl.when(has_b & out)
         def _():
             b_do(j, start)
 
-        @pl.when(has_b & (lax.rem(j + chunks, per) == per - 1))
-        def _():
-            by_out = jnp.concatenate([came[j - per + 1 + i] for i in range(per)], axis=0)
-            for c in blocks(ff):
-                acc[0, :, c] += mm_tn(a_all[...], by_gate[:, c]).astype(bf16).astype(f32)
-                acc[1, :, c] += mm_tn(a_all[...], by_up[:, c]).astype(bf16).astype(f32)
-                acc_down[c, :] += mm_tn(hid_all[:, c], by_out).astype(bf16).astype(f32)
-
         return 0
 
-    steps = chunks + jnp.maximum(lead, jnp.where(me == F_RELAY, F_BEHIND, jnp.where(me == B_RELAY, B_BEHIND, 0)))
+    steps = chunks + jnp.maximum(lead + 1, jnp.where(me == F_RELAY, F_BEHIND, jnp.where(me == B_RELAY, B_BEHIND, 0)))
     lax.fori_loop(0, steps, take, 0)
 
     def drain(i, _):
@@ -320,11 +346,11 @@
         chunks = micro * per
         x, dy = (v.reshape(chunks, ROWS, d) for v in (x, dy))
         vmem, anywhere = pl.BlockSpec(memory_space=pltpu.VMEM), pl.BlockSpec(memory_space=pl.ANY)
-        by_gate, by_up, by_down = pl.pallas_call(
+        by_gate, by_up, by_down, _ = pl.pallas_call(
             functools.partial(kernel, stages, chunks, per),
-            out_shape=[pltpu.VMEM((d, ff), bf16)] * 2 + [pltpu.VMEM((ff, d), bf16)],
+            out_shape=[pltpu.VMEM((d, ff), bf16)] * 2 + [pltpu.VMEM((ff, d), bf16), jax.ShapeDtypeStruct((chunks, 2, ROWS, ff), f32)],
             in_specs=[anywhere] * 2 + [vmem] * 3,
-            out_specs=[vmem] * 3,
+            out_specs=[vmem] * 3 + [anywhere],
             scratch_shapes=[
                 pltpu.VMEM((chunks, ROWS, d), bf16),
                 pltpu.VMEM((chunks, ROWS, d), bf16),
@@ -346,6 +372,8 @@
                 pltpu.SemaphoreType.DMA((chunks,)),
                 pltpu.SemaphoreType.DMA((chunks,)),
                 pltpu.SemaphoreType.DMA((RING,)),
+                pltpu.SemaphoreType.DMA((OUTGOING,)),
+                pltpu.SemaphoreType.DMA((INCOMING,)),
             ],
             compiler_params=pltpu.CompilerParams(collective_id=0, has_side_effects=True, vmem_limit_bytes=VMEM_BYTES),
             cost_estimate=pl.CostEstimate(flops=22 * micro * tokens * d * ff, bytes_accessed=16 * d * ff, transcendentals=0),

time: 212 us -> 207 us (0.976)
  Pallas kernels: 211 us -> 206 us
    pallas_call x1, Pallas kernels: 209 us -> 204 us  [step(): pl.pallas_call(functools.partial(kernel, stages, chunks, per), out_shape=...]
where the time goes in v3:
time: 207 us
  Pallas kernels  206 us (100%)
    pallas_call x1, Pallas kernels, step(): pl.pallas_call(functools.partial(kernel, stages, chunks, per), out_shape=...  204 us

profile of v3, /device:TPU:0, one launch (start us, length us, event | category | flops | bytes accessed | tf_op | source)
XLA Modules:
  0.0 206.5 jit_solution(12735745044832025129)
XLA Ops:
  0.6 203.9 %shard_map.76 = (bf16[512,1280]{1,0:T(8,128)(2,1)S(1)}, bf16[512,1280]{1,0:T(8,128)(2,1)S(1)}, bf16[1280,512]{1,0:T(8,128)(2,1)S(1)}, f32[32,2,256,1280]{3,2,1,0:T(8,128)}) custom-call(bf16[32,256,512]{2,1,0:T(8,128)(2,1)} %bitcast.8, bf16[32,256,512]{2,1,0:T(8,128)(2,1)} %bitcast.9, bf16[512,1280]{1,0:T(8,128)(2,1)} %bitcast.10, ...), custom_call_target="tpu_custom_call" | custom-call | flops 118111600640 | bytes 10485760 | tf_op jit(solution)/shard_map/pallas_call | solution.py:349
  204.6 1.9 shard_map.77

commit v4 on v3

--- a/solution.py
+++ b/solution.py
@@ -19,8 +19,8 @@
 F_SPLIT, B_SPLIT = (7, 31), (0, 20)
 F_BEHIND, B_BEHIND = 10, 6
 COVERED = ()
-STASHED, SLOTS = (1, 2, 3, 4, 5, 6), 9
-AWAY, OUTGOING, INCOMING, SOON = (1, 2, 3), 4, 4, 3
+STASHED, SLOTS = (1, 2, 3, 4, 5, 6), 7
+AWAY, OUTGOING, INCOMING, SOON = (1, 2, 3, 4), 3, 4, 3
 VMEM_BYTES = 60 * 2**20
 
 
@@ -45,29 +45,35 @@
     return [slice(at, at + BLOCK) for at in range(0, ff, BLOCK)]
 
 
-def forward(h, wg, wu, wd, hidden, stash=None):
+def forward(h, wg, wu, wd, stash, hidden):
     wide, scale = norm_of(h)
     a = (wide * scale).astype(bf16)
     for c in blocks(hidden.shape[1]):
         gate, up = mm(a, wg[:, c]), mm(a, wu[:, c])
-        if stash is not None:
-            stash[0, :, c], stash[1, :, c] = gate, up
-        hidden[:, c] = (gate * jax.nn.sigmoid(gate) * up).astype(bf16)
+        sig = jax.nn.sigmoid(gate)
+        silu = gate * sig
+        stash[0, :, c], stash[1, :, c] = silu, up * (sig + silu * (1.0 - sig))
+        hidden[:, c] = (silu * up).astype(bf16)
     return h + mm(hidden[...], wd[...]).astype(bf16)
 
 
-def backward(h, by_y, wg, wu, wd, a_all, hid_all, by_gate, by_up, rows, stash=None):
+def backward(h, by_y, wg, wu, wd, a_all, hid_all, by_gate, by_up, rows, stash=None, hidden=None):
     wide, scale = norm_of(h)
     a = (wide * scale).astype(bf16)
     a_all[rows, :] = a
     for c in blocks(hid_all.shape[1]):
-        gate, up = (mm(a, wg[:, c]), mm(a, wu[:, c])) if stash is None else (stash[0, :, c], stash[1, :, c])
+        if stash is None:
+            gate, up = mm(a, wg[:, c]), mm(a, wu[:, c])
+            sig = jax.nn.sigmoid(gate)
+            silu = gate * sig
+            slope = up * (sig + silu * (1.0 - sig))
+            hid_all[rows, c] = (silu * up).astype(bf16)
+        else:
+            silu, slope = stash[0, :, c], stash[1, :, c]
+            hid_all[rows, c] = hidden[:, c]
         by_hid = mm_nt(by_y, wd[c, :]).astype(bf16).astype(f32)
-        sig = jax.nn.sigmoid(gate)
-        silu = gate * sig
-        hid_all[rows, c] = (silu * up).astype(bf16)
         by_up[rows, c] = (by_hid * silu).astype(bf16)
-        by_gate[rows, c] = ((by_hid * up) * (sig + silu * (1.0 - sig))).astype(bf16)
+        by_gate[rows, c] = (by_hid * slope).astype(bf16)
     return wide, scale
 
 
@@ -78,12 +84,12 @@
     return by_y + (by_a * scale - wide * (scale * scale * scale * inner)).astype(bf16)
 
 
-def kernel(stages, chunks, per, x, dy, wg, wu, wd, o_gate, o_up, o_down, store, kept, came, f_out, b_out, hidden, a_all, hid_all,
-           acc, acc_down, relay, stash, f_in, b_in, f_sent, b_sent, f_round, b_round, r_in, r_sent, x_sent, s_out, s_back):
+def kernel(stages, chunks, per, x, dy, wg, wu, wd, o_gate, o_up, o_down, store, store_hid, kept, came, f_out, b_out, hidden, a_all, hid_all,
+           acc, acc_down, relay, stash, f_in, b_in, f_sent, b_sent, f_round, b_round, r_in, r_sent, x_sent, s_out, s_back, h_out, h_back):
     me = lax.axis_index("pp")
     first, last = me == 0, me == stages - 1
     lead = sum(jnp.where(me == i, n, 0) for i, n in enumerate(LEAD))
-    ff = hidden.shape[1]
+    ff = hid_all.shape[1]
     by_gate, by_up = o_gate, o_up
 
     barrier = pltpu.get_barrier_semaphore()
@@ -226,19 +232,27 @@
 
         def put(k):
             slot = lax.rem(k, OUTGOING)
-            return pltpu.make_async_copy(stash.at[slot], store.at[k], s_out.at[slot])
+            return (
+                pltpu.make_async_copy(stash.at[slot], store.at[k], s_out.at[slot]),
+                pltpu.make_async_copy(hidden.at[slot], store_hid.at[k], h_out.at[slot]),
+            )
 
         def get(j):
             slot = lax.rem(j, INCOMING)
-            return pltpu.make_async_copy(store.at[j], stash.at[OUTGOING + slot], s_back.at[slot])
+            return (
+                pltpu.make_async_copy(store.at[j], stash.at[OUTGOING + slot], s_back.at[slot]),
+                pltpu.make_async_copy(store_hid.at[j], hidden.at[OUTGOING + slot], h_back.at[slot]),
+            )
 
         @pl.when(away & (k >= OUTGOING) & (k < chunks + OUTGOING))
         def _():
-            put(k - OUTGOING).wait()
+            for copy in put(k - OUTGOING):
+                copy.wait()
 
         @pl.when(away & (j + SOON >= 0) & (j + SOON < chunks))
         def _():
-            get(j + SOON).start()
+            for copy in get(j + SOON):
+                copy.start()
 
         covered = due & has_f & covers
         pl.when(due & jnp.logical_not(covered))(weights)
@@ -260,16 +274,17 @@
 
             @pl.when(away)
             def _():
-                get(j).wait()
+                for copy in get(j):
+                    copy.wait()
 
         def work(forth, back, whole=True, stashed=False):
             if back:
-                kept_of = stash.at[b_slot] if stashed else None
-                wide, scale = backward(kept[j], came[j], wg, wu, wd, a_all, hid_all, by_gate, by_up, rows, kept_of)
+                kept_of = (stash.at[b_slot], hidden.at[b_slot]) if stashed else ()
+                wide, scale = backward(kept[j], came[j], wg, wu, wd, a_all, hid_all, by_gate, by_up, rows, *kept_of)
                 if whole:
                     b_out[lax.rem(j, RING)] = backward_input(wide, scale, came[j], wg, wu, by_gate, by_up, rows)
             if forth:
-                f_out[lax.rem(k, RING)] = forward(kept[k], wg, wu, wd, hidden, stash.at[f_slot] if stashed else None)
+                f_out[lax.rem(k, RING)] = forward(kept[k], wg, wu, wd, stash.at[f_slot], hidden.at[f_slot])
 
         @pl.when(covered)
         def _():
@@ -284,7 +299,8 @@
 
         @pl.when(has_f & away)
         def _():
-            put(k).start()
+            for copy in put(k):
+                copy.start()
 
         pl.when(has_b)(await_b)
         pl.when(has_b & first)(lambda: work(False, True, whole=False))
@@ -346,17 +362,17 @@
         chunks = micro * per
         x, dy = (v.reshape(chunks, ROWS, d) for v in (x, dy))
         vmem, anywhere = pl.BlockSpec(memory_space=pltpu.VMEM), pl.BlockSpec(memory_space=pl.ANY)
-        by_gate, by_up, by_down, _ = pl.pallas_call(
+        by_gate, by_up, by_down, *_ = pl.pallas_call(
             functools.partial(kernel, stages, chunks, per),
-            out_shape=[pltpu.VMEM((d, ff), bf16)] * 2 + [pltpu.VMEM((ff, d), bf16), jax.ShapeDtypeStruct((chunks, 2, ROWS, ff), f32)],
+            out_shape=[pltpu.VMEM((d, ff), bf16)] * 2 + [pltpu.VMEM((ff, d), bf16), jax.ShapeDtypeStruct((chunks, 2, ROWS, ff), f32), jax.ShapeDtypeStruct((chunks, ROWS, ff), bf16)],
             in_specs=[anywhere] * 2 + [vmem] * 3,
-            out_specs=[vmem] * 3 + [anywhere],
+            out_specs=[vmem] * 3 + [anywhere] * 2,
             scratch_shapes=[
                 pltpu.VMEM((chunks, ROWS, d), bf16),
                 pltpu.VMEM((chunks, ROWS, d), bf16),
                 pltpu.VMEM((RING, ROWS, d), bf16),
                 pltpu.VMEM((RING, ROWS, d), bf16),
-                pltpu.VMEM((ROWS, ff), bf16),
+                pltpu.VMEM((SLOTS, ROWS, ff), bf16),
                 pltpu.VMEM((tokens, d), bf16),
                 pltpu.VMEM((tokens, ff), bf16),
                 pltpu.VMEM((2, d, ff), f32),
@@ -372,6 +388,8 @@
                 pltpu.SemaphoreType.DMA((chunks,)),
                 pltpu.SemaphoreType.DMA((chunks,)),
                 pltpu.SemaphoreType.DMA((RING,)),
+                pltpu.SemaphoreType.DMA((OUTGOING,)),
+                pltpu.SemaphoreType.DMA((INCOMING,)),
                 pltpu.SemaphoreType.DMA((OUTGOING,)),
                 pltpu.SemaphoreType.DMA((INCOMING,)),
             ],

time: 207 us -> 204 us (0.986)
  Pallas kernels: 206 us -> 203 us
    pallas_call x1, Pallas kernels: 204 us -> 201 us  [step(): pl.pallas_call(functools.partial(kernel, stages, chunks, per), out_shape=...]
where the time goes in v4:
time: 204 us
  Pallas kernels  203 us (100%)
    pallas_call x1, Pallas kernels, step(): pl.pallas_call(functools.partial(kernel, stages, chunks, per), out_shape=...  201 us

profile of v4, /device:TPU:0, one launch (start us, length us, event | category | flops | bytes accessed | tf_op | source)
XLA Modules:
  0.0 203.7 jit_solution(15522275630780875395)
XLA Ops:
  0.6 201.1 %shard_map.76 = (bf16[512,1280]{1,0:T(8,128)(2,1)S(1)}, bf16[512,1280]{1,0:T(8,128)(2,1)S(1)}, bf16[1280,512]{1,0:T(8,128)(2,1)S(1)}, f32[32,2,256,1280]{3,2,1,0:T(8,128)}, bf16[32,256,1280]{2,1,0:T(8,128)(2,1)}) custom-call(bf16[32,256,512]{2,1,0:T(8,128)(2,1)} %bitcast.8, bf16[32,256,512]{2,1,0:T(8,128)(2,1)} %bitcast.9, bf16[512,1280]{1,0:T(8,128)(2,1)} %bitcast.10, ...), custom_call_target="tpu_custom_call" | custom-call | flops 118111600640 | bytes 10485760 | tf_op jit(solution)/shard_map/pallas_call | solution.py:365
  201.8 1.9 shard_map.77
